TPU v7x, 32 devices: a whole 2x2x4 slice. The times are simulated.
32 devices in a mesh: dp: 16 (over z, y, x), seq: 2 (over core).
Axes of the slice: x: 2, y: 2, z: 4, core: 2. Of those that a mesh axis runs over, the one named last changes fastest.
Arguments:
- activations: bfloat16 [4096, 8192], P(('dp', 'seq')), may hold values from -6 to 6
- queries: bfloat16 [4096, 8192], P(('dp', 'seq')), may hold values from -180 to 180
- keys: bfloat16 [4096, 1024], P(('dp', 'seq')), may hold values from -6 to 6
- out_grad: bfloat16 [4096, 8192], P(('dp', 'seq')), may hold values from -0.078125 to 0.078125
- layout: int32 [8192], replicated, may hold values from 0 to 8191, each once
Outputs:
- value_weight_grad: float32 [8192, 1024], P(('dp', 'seq'))
Inputs may be any that keep to these rules, and one draw needn't show every extreme that they name: `layout`: every row number 0 to 8191 appears exactly once.
All inputs are finite; a program needn't handle non-finite values.
Results may differ from a plain program's by a relative error of at most 0.0049.
Values may be sent and summed in bfloat16 or wider, within the bound.
A program may use at most 128 MiB of HBM per device.

v0:
```python
import functools
import math

import jax
import jax.numpy as jnp
from jax import lax
from jax.experimental import pallas as pl
from jax.experimental.pallas import tpu as pltpu
from jax.sharding import PartitionSpec as P

H = 64
KVH = 8
HD = 128
SEQ = 2
CHUNK = 256
MESH = pl.DeviceIdType.MESH


def relative(place, step, bits):
    total = 0
    for b in range(bits):
        total = total + (place // (1 << b) + step // (1 << b)) % 2 * (1 << b)
    return total


def turn(z, k, count):
    above = count - 1 - z
    sign = jnp.where(above >= z, 1, -1)
    big, small = jnp.maximum(above, z), jnp.minimum(above, z)
    later = k - (big - small)
    lone = later < 0
    distance = jnp.where(lone, big - k, small - later // 2)
    side = jnp.where(lone | (later % 2 == 1), sign, -sign)
    return z + side * distance


def fused_kernel(
    act_hbm, q_hbm, k_hbm, grad_hbm, layout_hbm, out_ref,
    act, flipped, picked, lay, qb, kb, gb, send, held, vg, down_in, up_in, part, acc,
    load_sem, swap_send, swap_recv, a2a_send, a2a_recv, ag_send, ag_recv,
    fwd_send, fwd_recv, rs_send, up_sem, down_sem, *, planes, inner,
):
    tokens, width = act_hbm.shape
    rows = out_ref.shape[0]
    bits = inner.bit_length() - 1
    me, core = lax.axis_index("dp"), lax.axis_index("seq")
    z, p = me // inner, me % inner
    other = 1 - core
    heads_cols, key_cols = q_hbm.shape[1] // SEQ, k_hbm.shape[1] // SEQ
    length = SEQ * tokens
    per_group = H // KVH
    chunks_core = key_cols // CHUNK
    chunks = SEQ * chunks_core
    place = p * SEQ + core

    loads = [
        pltpu.make_async_copy(act_hbm, act, load_sem.at[0]),
        pltpu.make_async_copy(layout_hbm, lay, load_sem.at[1]),
    ]
    for i, (source, target, cols) in enumerate(
        ((k_hbm, kb, key_cols), (q_hbm, qb, heads_cols), (grad_hbm, gb, heads_cols))
    ):
        loads.append(
            pltpu.make_async_copy(
                source.at[:, pl.ds(pl.multiple_of(core * cols, 128), cols)],
                target.at[pl.ds(pl.multiple_of(core * tokens, 128), tokens), :],
                load_sem.at[2 + i],
            )
        )
    for load in loads:
        load.start()

    barrier = pltpu.get_barrier_semaphore()
    for j in range(1, inner * SEQ):
        to = (z * inner + relative(p, j // SEQ, bits), (core + j) % SEQ)
        pl.semaphore_signal(barrier, inc=1, device_id=to, device_id_type=MESH)

    @pl.when(z > 0)
    def _():
        pl.semaphore_signal(barrier, inc=1, device_id=(me - inner, core), device_id_type=MESH)

    @pl.when(z < planes - 1)
    def _():
        pl.semaphore_signal(barrier, inc=1, device_id=(me + inner, core), device_id_type=MESH)

    near = inner * SEQ - 1 + jnp.where(z > 0, 1, 0) + jnp.where(z < planes - 1, 1, 0)
    pl.semaphore_wait(barrier, near)

    swaps = []
    for i, (source, target, cols) in enumerate(
        ((k_hbm, kb, key_cols), (q_hbm, qb, heads_cols), (grad_hbm, gb, heads_cols))
    ):
        swaps.append(
            pltpu.make_async_remote_copy(
                src_ref=source.at[:, pl.ds(pl.multiple_of(other * cols, 128), cols)],
                dst_ref=target.at[pl.ds(pl.multiple_of(core * tokens, 128), tokens), :],
                send_sem=swap_send.at[i],
                recv_sem=swap_recv.at[i],
                device_id=(me, other),
                device_id_type=MESH,
            )
        )
    for swap in swaps:
        swap.start()

    loads[0].wait()
    step = 512

    def flip(i, carry):
        at = pl.multiple_of(i * step, step)
        flipped[pl.ds(at, step), :] = act[:, pl.ds(at, step)].astype(jnp.float32).T
        return carry

    lax.fori_loop(0, width // step, flip, 0)
    loads[1].wait()

    def pick(first_row):
        def some(i, carry):
            first = pl.multiple_of(i * 32, 32)
            for r in range(32):
                row = lay[first_row + first + r]
                picked[pl.ds(first + r, 1), :] = flipped[pl.ds(row, 1), :]
            return carry

        lax.fori_loop(0, rows // 32, some, 0)

    def block(k, j):
        to_p, to_core = relative(p, j // SEQ, bits), (core + j) % SEQ
        owner = turn(z, k, planes)
        return pltpu.make_async_remote_copy(
            src_ref=send.at[k, j],
            dst_ref=held.at[owner, :, pl.ds(pl.multiple_of(place * tokens, 128), tokens)],
            send_sem=a2a_send.at[k, j],
            recv_sem=a2a_recv.at[k, j],
            device_id=(z * inner + to_p, to_core),
            device_id_type=MESH,
        )

    def gather_step(k):
        owner = turn(z, k, planes)

        def to(j, carry):
            to_p, to_core = relative(p, j // SEQ, bits), (core + j) % SEQ
            pick(((owner * inner + to_p) * SEQ + to_core) * rows)
            send[k, j] = picked[...].astype(jnp.bfloat16)
            block(k, j).start()
            return carry

        lax.fori_loop(1, inner * SEQ, to, 0)
        pick(((owner * inner + p) * SEQ + core) * rows)
        held[owner, :, pl.ds(pl.multiple_of(place * tokens, 128), tokens)] = picked[...].astype(jnp.bfloat16)

    gather_step(0)

    for load in loads[2:]:
        load.wait()
    for swap in swaps:
        swap.wait_recv()
    scale = math.log2(math.e) / float(HD) ** 0.5
    key_at = lax.broadcasted_iota(jnp.int32, (tokens, 2 * tokens), 0)
    query_at = lax.broadcasted_iota(jnp.int32, (tokens, 2 * tokens), 1) % tokens
    allowed = key_at <= query_at

    def weights_of(scores):
        powers = jnp.exp2((scores - jnp.max(scores, axis=0, keepdims=True)) * scale)
        return (powers * (1.0 / jnp.sum(powers, axis=0, keepdims=True))).astype(jnp.bfloat16)

    def stacked(ref, row, col):
        return jnp.concatenate(
            [
                ref[row : row + tokens, pl.ds(pl.multiple_of(col, 128), HD)],
                ref[row : row + tokens, pl.ds(pl.multiple_of(col + HD, 128), HD)],
            ],
            axis=0,
        )

    def attend(g):
        keys = kb[:, pl.ds(pl.multiple_of(g * HD, 128), HD)]
        early = jnp.zeros((tokens, HD), jnp.float32)
        both = jnp.zeros((length, HD), jnp.float32)
        for pair in range(per_group // 2):
            col = (g * per_group + 2 * pair) * HD
            against = (((1,), (1,)), ((), ()))
            first = lax.dot_general(
                keys[:tokens], stacked(qb, 0, col), against, preferred_element_type=jnp.float32
            )
            second = lax.dot_general(
                keys, stacked(qb, tokens, col), against, preferred_element_type=jnp.float32
            )
            first = jnp.where(allowed, first, -jnp.inf)
            second = jnp.concatenate(
                [second[:tokens], jnp.where(allowed, second[tokens:], -jnp.inf)], axis=0
            )
            early += jnp.dot(
                weights_of(first), stacked(gb, 0, col), preferred_element_type=jnp.float32
            )
            both += jnp.dot(
                weights_of(second), stacked(gb, tokens, col), preferred_element_type=jnp.float32
            )
        done = jnp.concatenate([both[:tokens] + early, both[tokens:]], axis=0)
        vg[
            pl.ds(pl.multiple_of(p * length, 128), length),
            pl.ds(pl.multiple_of(core * key_cols + g * HD, 128), HD),
        ] = done.astype(jnp.bfloat16)

    def grads(from_p, from_core, c):
        return vg.at[
            pl.ds(pl.multiple_of(from_p * length, 128), length),
            pl.ds(pl.multiple_of(from_core * key_cols + c * CHUNK, 128), CHUNK),
        ]

    def gather_copy(c, jp):
        return pltpu.make_async_remote_copy(
            src_ref=grads(p, core, c), dst_ref=grads(p, core, c),
            send_sem=ag_send.at[c, jp], recv_sem=ag_recv.at[c, jp],
            device_id=(z * inner + relative(p, jp, bits), core), device_id_type=MESH,
        )

    def forward_copy(c, jp):
        from_p = relative(p, jp, bits)
        return pltpu.make_async_remote_copy(
            src_ref=grads(from_p, core, c), dst_ref=grads(from_p, core, c),
            send_sem=fwd_send.at[c, jp], recv_sem=fwd_recv.at[c, jp],
            device_id=(me, other), device_id_type=MESH,
        )

    per_chunk = CHUNK // HD
    for c in range(chunks_core):
        lax.fori_loop(c * per_chunk, (c + 1) * per_chunk, lambda g, carry: (attend(g), carry)[1], 0)
        for jp in range(1, inner):
            gather_copy(c, jp).start()
        forward_copy(c, 0).start()

    def pass_on(c):
        for jp in range(1, inner):
            gather_copy(c, jp).wait_recv()
            forward_copy(c, jp).start()

    def arrived(c):
        for jp in range(inner):
            forward_copy(c, jp).wait_recv()

    def slot(ref, owner, q):
        return ref.at[owner, :, pl.ds(pl.multiple_of(q * CHUNK, 128), CHUNK)]

    def up_copy(owner, q):
        return pltpu.make_async_remote_copy(
            src_ref=slot(part, owner, q), dst_ref=slot(up_in, owner, q),
            send_sem=rs_send.at[owner, q], recv_sem=up_sem.at[owner, q],
            device_id=(me + inner, core), device_id_type=MESH,
        )

    def down_copy(owner, q):
        return pltpu.make_async_remote_copy(
            src_ref=slot(part, owner, q), dst_ref=slot(down_in, owner, q),
            send_sem=rs_send.at[owner, q], recv_sem=down_sem.at[owner, q],
            device_id=(me - inner, core), device_id_type=MESH,
        )

    def reduce_step(k, i):
        owner = turn(z, k, planes)
        q = i % SEQ * chunks_core + i // SEQ
        cols = pl.ds(pl.multiple_of(q * CHUNK, 128), CHUNK)
        acc[...] = jnp.dot(held[owner], vg[:, cols], preferred_element_type=jnp.float32)

        @pl.when((owner >= z) & (z > 0))
        def _():
            up_copy(owner, q).wait_recv()
            acc[...] += up_in[owner, :, cols].astype(jnp.float32)

        @pl.when((owner <= z) & (z < planes - 1))
        def _():
            down_copy(owner, q).wait_recv()
            acc[...] += down_in[owner, :, cols].astype(jnp.float32)

        @pl.when(owner == z)
        def _():
            out_ref[:, cols] = acc[...]

        @pl.when(owner != z)
        def _():
            part[owner, :, cols] = acc[...].astype(jnp.bfloat16)

        @pl.when(owner > z)
        def _():
            up_copy(owner, q).start()

        @pl.when(owner < z)
        def _():
            down_copy(owner, q).start()

    def reduce_steps(k, first, last):
        lax.fori_loop(first, last, lambda i, carry: (reduce_step(k, i), carry)[1], 0)

    def took(k):
        lax.fori_loop(1, inner * SEQ, lambda j, carry: (block(k, j).wait_recv(), carry)[1], 0)

    lax.fori_loop(1, planes - 1, lambda k, carry: (gather_step(k), carry)[1], 0)
    took(0)
    for c in range(chunks_core):
        pass_on(c)
        arrived(c)
        reduce_steps(0, c * SEQ, (c + 1) * SEQ)
        if c == 0:
            gather_step(planes - 1)

    def rest(k, carry):
        took(k)
        reduce_steps(k, 0, chunks)
        return carry

    lax.fori_loop(1, planes, rest, 0)

    for swap in swaps:
        swap.wait_send()

    def left(k, carry):
        lax.fori_loop(1, inner * SEQ, lambda j, inside: (block(k, j).wait_send(), inside)[1], 0)
        return carry

    lax.fori_loop(0, planes, left, 0)
    for c in range(chunks_core):
        for jp in range(inner):
            if jp:
                gather_copy(c, jp).wait_send()
            forward_copy(c, jp).wait_send()

    def sent(k, carry):
        owner = turn(z, k, planes)
        lax.fori_loop(0, chunks, lambda q, inside: (up_copy(owner, q).wait_send(), inside)[1], 0)
        return carry

    lax.fori_loop(0, planes - 1, sent, 0)


def body(activations, queries, keys, out_grad, layout):
    members = lax.axis_size("dp")
    tokens, width = activations.shape
    inner = 1 << ((members.bit_length() - 1) // 2)
    planes = members // inner
    rows = layout.shape[0] // (members * SEQ)
    kv_width = keys.shape[1]
    chunks_core = kv_width // SEQ // CHUNK
    chunks = SEQ * chunks_core
    length = SEQ * tokens
    anywhere = pl.BlockSpec(memory_space=pl.ANY)
    dma = pltpu.SemaphoreType.DMA
    return pl.pallas_call(
        functools.partial(fused_kernel, planes=planes, inner=inner),
        out_shape=jax.ShapeDtypeStruct((rows, kv_width), jnp.float32),
        in_specs=[anywhere] * 5,
        out_specs=pl.BlockSpec(memory_space=pltpu.VMEM),
        scratch_shapes=[
            pltpu.VMEM((tokens, width), jnp.bfloat16),
            pltpu.VMEM((width, tokens), jnp.float32),
            pltpu.VMEM((rows, tokens), jnp.float32),
            pltpu.SMEM(layout.shape, jnp.int32),
            pltpu.VMEM((length, queries.shape[1] // SEQ), jnp.bfloat16),
            pltpu.VMEM((length, kv_width // SEQ), jnp.bfloat16),
            pltpu.VMEM((length, queries.shape[1] // SEQ), jnp.bfloat16),
            pltpu.VMEM((planes, inner * SEQ, rows, tokens), jnp.bfloat16),
            pltpu.VMEM((planes, rows, inner * length), jnp.bfloat16),
            pltpu.VMEM((inner * length, kv_width), jnp.bfloat16),
            pltpu.VMEM((planes, rows, kv_width), jnp.bfloat16),
            pltpu.VMEM((planes, rows, kv_width), jnp.bfloat16),
            pltpu.VMEM((planes, rows, kv_width), jnp.bfloat16),
            pltpu.VMEM((rows, CHUNK), jnp.float32),
            dma((5,)),
            dma((3,)),
            dma((3,)),
            dma((planes, inner * SEQ)),
            dma((planes, inner * SEQ)),
            dma((chunks_core, inner)),
            dma((chunks_core, inner)),
            dma((chunks_core, inner)),
            dma((chunks_core, inner)),
            dma((planes, chunks)),
            dma((planes, chunks)),
            dma((planes, chunks)),
        ],
        compiler_params=pltpu.CompilerParams(
            collective_id=0, has_side_effects=True, vmem_limit_bytes=56 * 2**20
        ),
    )(activations, queries, keys, out_grad, layout)


def solution(mesh):
    whole = ("dp", "seq")
    return jax.shard_map(
        body,
        mesh=mesh,
        in_specs=(P(whole, None),) * 4 + (P(),),
        out_specs=P(whole, None),
        check_vma=False,
    )
```

profile of v0, /device:TPU:17, one launch (start us, length us, event | category | flops | bytes accessed | tf_op | source)
XLA Modules:
  0.0 61.5 jit_solution(2257399125082405168)
XLA Ops:
  0.0 59.2 %shard_map.55 = f32[256,1024]{1,0:T(8,128)} custom-call(bf16[128,8192]{1,0:T(8,128)(2,1)} %act_hbm.1, bf16[128,8192]{1,0:T(8,128)(2,1)} %q_hbm.1, bf16[128,1024]{1,0:T(8,128)(2,1)} %k_hbm.1, bf16[128,8192]{1,0:T(8,128)(2,1)} %grad_hbm.1, s32[8192]{0:T(1024)} %layout_hbm.1), custom_call_target="tpu_custom_call" | custom-call | tf_op jit(solution)/shard_map/pallas_call | solution.py:348
  59.2 2.3 %copy.7 = f32[256,1024]{1,0:T(8,128)} copy(f32[256,1024]{1,0:T(8,128)} %shard_map.55) | data formatting | bytes 2097152
where the time goes:
time: 61.7 us; the launch traced here: 61.5 us
  Pallas kernels  59.2 us (96%)
  local copies, waits for them, and re-layouts  2.31 us (4%)
    pallas_call x1, Pallas kernels, body(): pl.pallas_call(functools.partial(fused_kernel, planes=planes, inner=inner...  59.2 us
    unnamed x1, local copies, waits for them, and re-layouts  2.31 us

commit v1 on v0

v1 whole, which is shorter than its diff:
```python
import functools
import math

import jax
import jax.numpy as jnp
from jax import lax
from jax.experimental import pallas as pl
from jax.experimental.pallas import tpu as pltpu
from jax.sharding import PartitionSpec as P

H = 64
KVH = 8
HD = 128
SEQ = 2
MESH = pl.DeviceIdType.MESH


def relative(place, step, bits):
    total = 0
    for b in range(bits):
        total = total + (place // (1 << b) + step // (1 << b)) % 2 * (1 << b)
    return total


def turn(z, k, count):
    above = count - 1 - z
    sign = jnp.where(above >= z, 1, -1)
    big, small = jnp.maximum(above, z), jnp.minimum(above, z)
    later = k - (big - small)
    lone = later < 0
    distance = jnp.where(lone, big - k, small - later // 2)
    side = jnp.where(lone | (later % 2 == 1), sign, -sign)
    return z + side * distance


def fused_kernel(
    act_hbm, q_hbm, k_hbm, grad_hbm, layout_hbm, out_ref,
    act, flipped, picked, lay, qb, kb, gb, send, held, vg, down_in, up_in, part, acc,
    act_sem, lay_sem, load_sem, swap_send, swap_recv, a2a_send, a2a_recv, ag_send, ag_recv,
    fwd_send, fwd_recv, rs_send, line_sem, *, planes, inner,
):
    tokens, width = act_hbm.shape
    rows = out_ref.shape[0]
    bits = inner.bit_length() - 1
    me, core = lax.axis_index("dp"), lax.axis_index("seq")
    z, p = me // inner, me % inner
    other = 1 - core
    heads_cols, key_cols = q_hbm.shape[1] // SEQ, k_hbm.shape[1] // SEQ
    length = SEQ * tokens
    per_group = H // KVH
    groups = key_cols // HD
    half = rows // 2
    place = p * SEQ + core
    group_cols = per_group * HD
    stretch = width // 4

    cuts = ((k_hbm, kb, key_cols, 0, key_cols),) + tuple(
        (source, target, heads_cols, first, last - first)
        for first, last in ((0, group_cols), (group_cols, heads_cols))
        for source, target in ((q_hbm, qb), (grad_hbm, gb))
    )

    early_cuts = 3

    def cut(i, of_core):
        source, target, cols, first, count = cuts[i]
        return (
            source.at[:, pl.ds(pl.multiple_of(of_core * cols + first, 128), count)],
            target.at[pl.ds(pl.multiple_of(core * tokens, 128), tokens), pl.ds(first, count)],
        )

    flips = [
        pltpu.make_async_copy(
            act_hbm.at[:, pl.ds(i * stretch, stretch)],
            act.at[:, pl.ds(i * stretch, stretch)],
            act_sem.at[i],
        )
        for i in range(width // stretch)
    ]
    lay_load = pltpu.make_async_copy(layout_hbm, lay, lay_sem)
    loads = [pltpu.make_async_copy(*cut(i, core), load_sem.at[i]) for i in range(len(cuts))]
    for load in [*flips, lay_load, *loads]:
        load.start()

    barrier = pltpu.get_barrier_semaphore()
    for j in range(1, inner * SEQ):
        to = (z * inner + relative(p, j // SEQ, bits), (core + j) % SEQ)
        pl.semaphore_signal(barrier, inc=1, device_id=to, device_id_type=MESH)

    @pl.when(z > 0)
    def _():
        pl.semaphore_signal(barrier, inc=1, device_id=(me - inner, core), device_id_type=MESH)

    @pl.when(z < planes - 1)
    def _():
        pl.semaphore_signal(barrier, inc=1, device_id=(me + inner, core), device_id_type=MESH)

    near = inner * SEQ - 1 + jnp.where(z > 0, 1, 0) + jnp.where(z < planes - 1, 1, 0)
    with jax.named_scope('barrier'):
        pl.semaphore_wait(barrier, near)

    swaps = []
    for i in range(len(cuts)):
        source, target = cut(i, other)
        swaps.append(
            pltpu.make_async_remote_copy(
                src_ref=source, dst_ref=target, send_sem=swap_send, recv_sem=swap_recv.at[int(i >= early_cuts)],
                device_id=(me, other), device_id_type=MESH,
            )
        )
    for swap in swaps:
        swap.start()

    step = 512

    def flip(i, carry):
        at = pl.multiple_of(i * step, step)
        flipped[pl.ds(at, step), :] = act[:, pl.ds(at, step)].T.astype(jnp.float32)
        return carry

    for i, load in enumerate(flips):
        with jax.named_scope("act_wait"):
            load.wait()
        with jax.named_scope("flip"):
            lax.fori_loop(i * stretch // step, (i + 1) * stretch // step, flip, 0)
    lay_load.wait()

    def wait_for(like, sem):
        pltpu.make_async_remote_copy(
            src_ref=like, dst_ref=like, send_sem=sem, recv_sem=sem,
            device_id=(me, other), device_id_type=MESH,
        ).wait_recv()

    def pick(first_row):
        def some(i, carry):
            first = pl.multiple_of(i * 32, 32)
            for r in range(32):
                row = lay[first_row + first + r]
                picked[pl.ds(first + r, 1), :] = flipped[pl.ds(row, 1), :]
            return carry

        lax.fori_loop(0, half // 32, some, 0)

    def held_piece(owner, h):
        return held.at[
            owner,
            pl.ds(pl.multiple_of(h * half, 16), half),
            pl.ds(pl.multiple_of(place * tokens, 128), tokens),
        ]

    def block(k, h, j):
        to_p, to_core = relative(p, j // SEQ, bits), (core + j) % SEQ
        return pltpu.make_async_remote_copy(
            src_ref=send.at[k, j, pl.ds(pl.multiple_of(h * half, 16), half)],
            dst_ref=held_piece(turn(z, k, planes), h),
            send_sem=a2a_send,
            recv_sem=a2a_recv.at[k, h],
            device_id=(z * inner + to_p, to_core),
            device_id_type=MESH,
        )

    def gather(k, h):
        owner = turn(z, k, planes)

        def first_row(to_p, to_core):
            return ((owner * inner + to_p) * SEQ + to_core) * rows + h * half

        def to(j, carry):
            pick(first_row(relative(p, j // SEQ, bits), (core + j) % SEQ))
            send[k, j, pl.ds(pl.multiple_of(h * half, 16), half)] = picked[...].astype(jnp.bfloat16)
            block(k, h, j).start()
            return carry

        lax.fori_loop(1, inner * SEQ, to, 0)
        pick(first_row(p, core))
        held_piece(owner, h)[...] = picked[...].astype(jnp.bfloat16)

    def took(k, h):
        wait_for(send.at[0, 1:, :half], a2a_recv.at[k, h])

    scale = math.log2(math.e) / float(HD) ** 0.5
    key_at = lax.broadcasted_iota(jnp.int32, (tokens, 2 * tokens), 0)
    query_at = lax.broadcasted_iota(jnp.int32, (tokens, 2 * tokens), 1) % tokens
    allowed = key_at <= query_at

    def weights_of(scores):
        powers = jnp.exp2((scores - jnp.max(scores, axis=0, keepdims=True)) * scale)
        return (powers * (1.0 / jnp.sum(powers, axis=0, keepdims=True))).astype(jnp.bfloat16)

    def stacked(ref, row, col):
        return jnp.concatenate(
            [
                ref[row : row + tokens, pl.ds(pl.multiple_of(col, 128), HD)],
                ref[row : row + tokens, pl.ds(pl.multiple_of(col + HD, 128), HD)],
            ],
            axis=0,
        )

    def grads(from_p, from_core, g):
        return vg.at[
            pl.ds(pl.multiple_of(from_p * length, 128), length),
            pl.ds(pl.multiple_of((g * SEQ + from_core) * HD, 128), HD),
        ]

    def attend(g):
        keys = kb[:, pl.ds(pl.multiple_of(g * HD, 128), HD)]
        early = jnp.zeros((tokens, HD), jnp.float32)
        both = jnp.zeros((length, HD), jnp.float32)
        for pair in range(per_group // 2):
            col = (g * per_group + 2 * pair) * HD
            against = (((1,), (1,)), ((), ()))
            first = lax.dot_general(
                keys[:tokens], stacked(qb, 0, col), against, preferred_element_type=jnp.float32
            )
            second = lax.dot_general(
                keys, stacked(qb, tokens, col), against, preferred_element_type=jnp.float32
            )
            first = jnp.where(allowed, first, -jnp.inf)
            second = jnp.concatenate(
                [second[:tokens], jnp.where(allowed, second[tokens:], -jnp.inf)], axis=0
            )
            early += jnp.dot(
                weights_of(first), stacked(gb, 0, col), preferred_element_type=jnp.float32
            )
            both += jnp.dot(
                weights_of(second), stacked(gb, tokens, col), preferred_element_type=jnp.float32
            )
        done = jnp.concatenate([both[:tokens] + early, both[tokens:]], axis=0)
        grads(p, core, g)[...] = done.astype(jnp.bfloat16)

    def gather_copy(g, jp):
        return pltpu.make_async_remote_copy(
            src_ref=grads(p, core, g), dst_ref=grads(p, core, g),
            send_sem=ag_send, recv_sem=ag_recv.at[g],
            device_id=(z * inner + relative(p, jp, bits), core), device_id_type=MESH,
        )

    def forward_copy(g, jp):
        piece = grads(relative(p, jp, bits), core, g)
        return pltpu.make_async_remote_copy(
            src_ref=piece, dst_ref=piece,
            send_sem=fwd_send, recv_sem=fwd_recv.at[g],
            device_id=(me, other), device_id_type=MESH,
        )

    def publish(g):
        attend(g)
        for jp in range(1, inner):
            gather_copy(g, jp).start()
        forward_copy(g, 0).start()

    def pass_on(g):
        wait_for(vg.at[: (inner - 1) * length, :HD], ag_recv.at[g])
        for jp in range(1, inner):
            forward_copy(g, jp).start()

    def arrived(g):
        wait_for(vg.at[:, :HD], fwd_recv.at[g])

    def slot(ref, owner, h, g):
        return ref.at[
            owner,
            pl.ds(pl.multiple_of(h * half, 16), half),
            pl.ds(pl.multiple_of(g * SEQ * HD, 128), SEQ * HD),
        ]

    def up_copy(owner, h, g):
        return pltpu.make_async_remote_copy(
            src_ref=slot(part, owner, h, g), dst_ref=slot(up_in, owner, h, g),
            send_sem=rs_send, recv_sem=line_sem.at[owner, h, g],
            device_id=(me + inner, core), device_id_type=MESH,
        )

    def down_copy(owner, h, g, at):
        return pltpu.make_async_remote_copy(
            src_ref=slot(part, owner, h, g), dst_ref=slot(down_in, owner, h, g),
            send_sem=rs_send, recv_sem=line_sem.at[jnp.where(owner == at, planes, owner), h, g],
            device_id=(me - inner, core), device_id_type=MESH,
        )

    def reduce(k, h, g):
        owner = turn(z, k, planes)
        at_rows = pl.ds(pl.multiple_of(h * half, 16), half)
        cols = pl.ds(pl.multiple_of(g * SEQ * HD, 128), SEQ * HD)
        acc[...] = jnp.dot(held[owner, at_rows, :], vg[:, cols], preferred_element_type=jnp.float32)

        @pl.when((owner >= z) & (z > 0))
        def _():
            up_copy(owner, h, g).wait_recv()
            acc[...] += slot(up_in, owner, h, g)[...].astype(jnp.float32)

        @pl.when((owner <= z) & (z < planes - 1))
        def _():
            down_copy(owner, h, g, z).wait_recv()
            acc[...] += slot(down_in, owner, h, g)[...].astype(jnp.float32)

        @pl.when(owner == z)
        def _():
            for c in range(SEQ):
                out_ref[at_rows, pl.ds(pl.multiple_of((c * groups + g) * HD, 128), HD)] = acc[
                    :, c * HD : (c + 1) * HD
                ]

        @pl.when(owner != z)
        def _():
            slot(part, owner, h, g)[...] = acc[...].astype(jnp.bfloat16)

        @pl.when(owner > z)
        def _():
            up_copy(owner, h, g).start()

        @pl.when(owner < z)
        def _():
            down_copy(owner, h, g, z - 1).start()

    def each(first, last, step):
        lax.fori_loop(first, last, lambda i, carry: (step(i), carry)[1], 0)

    with jax.named_scope("g00"):
        gather(0, 0)
    with jax.named_scope("qwait"):
        for load in loads[:early_cuts]:
            load.wait()
        wait_for(qb.at[:tokens, : 2 * group_cols + key_cols], swap_recv.at[0])
    with jax.named_scope("a0"):
        publish(0)
    with jax.named_scope("g01"):
        gather(0, 1)
    with jax.named_scope("qwait2"):
        for load in loads[early_cuts:]:
            load.wait()
        wait_for(qb.at[:, group_cols:], swap_recv.at[1])
    with jax.named_scope("a123"):
        each(1, groups, publish)
    for g in range(groups):
        with jax.named_scope(f"pass{g}"):
            pass_on(g)
        if g < 2 * (planes - 1):
            with jax.named_scope(f"ga{g}"):
                gather(1 + g // 2, g % 2)
        if g == 0:
            with jax.named_scope("took00"):
                took(0, 0)
        with jax.named_scope(f"arr{g}"):
            arrived(g)
        with jax.named_scope(f"red0_{g}"):
            reduce(0, 0, g)
            if g == 0:
                with jax.named_scope("took01"):
                    took(0, 1)
            reduce(0, 1, g)
    with jax.named_scope("glast"):
        each(groups, 2 * (planes - 1), lambda i: gather(1 + i // 2, i % 2))

    def rest(i):
        with jax.named_scope("took"):
            took(i // 2, i % 2)
        with jax.named_scope("red"):
            each(0, groups, lambda g: reduce(i // 2, i % 2, g))

    each(2, 2 * planes, rest)

    with jax.named_scope("t0"):
        for ref in (qb, gb, kb):
            wait_for(ref.at[:tokens], swap_send)
        wait_for(send.at[:, 1:], a2a_send)
        wait_for(vg.at[: (inner - 1) * length, : groups * HD], ag_send)
        wait_for(vg.at[:, : groups * HD], fwd_send)
    with jax.named_scope("t3"):
        wait_for(part.at[1:], rs_send)


def body(activations, queries, keys, out_grad, layout):
    members = lax.axis_size("dp")
    tokens, width = activations.shape
    inner = 1 << ((members.bit_length() - 1) // 2)
    planes = members // inner
    rows = layout.shape[0] // (members * SEQ)
    kv_width = keys.shape[1]
    groups = kv_width // SEQ // HD
    length = SEQ * tokens
    dma = pltpu.SemaphoreType.DMA
    operands = (activations, queries, keys, out_grad, layout)
    return pl.pallas_call(
        functools.partial(fused_kernel, planes=planes, inner=inner),
        out_shape=jax.ShapeDtypeStruct((rows, kv_width), jnp.float32),
        in_specs=[pl.BlockSpec(memory_space=pltpu.HBM)] * len(operands),
        out_specs=pl.BlockSpec(memory_space=pltpu.VMEM),
        scratch_shapes=[
            pltpu.VMEM((tokens, width), jnp.bfloat16),
            pltpu.VMEM((width, tokens), jnp.float32),
            pltpu.VMEM((rows // 2, tokens), jnp.float32),
            pltpu.SMEM(layout.shape, jnp.int32),
            pltpu.VMEM((length, queries.shape[1] // SEQ), jnp.bfloat16),
            pltpu.VMEM((length, kv_width // SEQ), jnp.bfloat16),
            pltpu.VMEM((length, queries.shape[1] // SEQ), jnp.bfloat16),
            pltpu.VMEM((planes, inner * SEQ, rows, tokens), jnp.bfloat16),
            pltpu.VMEM((planes, rows, inner * length), jnp.bfloat16),
            pltpu.VMEM((inner * length, kv_width), jnp.bfloat16),
            pltpu.VMEM((planes, rows, kv_width), jnp.bfloat16),
            pltpu.VMEM((planes, rows, kv_width), jnp.bfloat16),
            pltpu.VMEM((planes, rows, kv_width), jnp.bfloat16),
            pltpu.VMEM((rows // 2, SEQ * HD), jnp.float32),
            dma((4,)),
            dma(()),
            dma((5,)),
            dma(()),
            dma((2,)),
            dma(()),
            dma((planes, 2)),
            dma(()),
            dma((groups,)),
            dma(()),
            dma((groups,)),
            dma(()),
            dma((planes + 1, 2, groups)),
        ],
        compiler_params=pltpu.CompilerParams(
            collective_id=0, has_side_effects=True, vmem_limit_bytes=32 * 2**20
        ),
    )(*(pltpu.with_memory_space_constraint(x, pltpu.HBM) for x in operands))


def solution(mesh):
    whole = ("dp", "seq")
    return jax.shard_map(
        body,
        mesh=mesh,
        in_specs=(P(whole, None),) * 4 + (P(),),
        out_specs=P(whole, None),
        check_vma=False,
    )
```

time: 61.7 us -> 55.2 us (0.89)
  Pallas kernels: 59.2 us -> 53.8 us
  local copies, waits for them, and re-layouts: 2.31 us -> 0.97 us
    pallas_call x1, Pallas kernels: 59.2 us -> 53.8 us  [body(): pl.pallas_call(functools.partial(fused_kernel, planes=planes, inner=inner...]
    unnamed x1, local copies, waits for them, and re-layouts: 2.31 us -> 0.97 us
where the time goes in v1:
time: 55.2 us; the launch traced here: 54.8 us
  Pallas kernels  53.8 us (97%)
  local copies, waits for them, and re-layouts  0.97 us (2%)
    pallas_call x1, Pallas kernels, body(): pl.pallas_call(functools.partial(fused_kernel, planes=planes, inner=inner...  53.8 us

profile of v1, /device:TPU:17, one launch (start us, length us, event | category | flops | bytes accessed | tf_op | source)
XLA Modules:
  0.0 54.8 jit_solution(9730581217956275597)
XLA Ops:
  0.0 53.8 %shard_map.55 = f32[256,1024]{1,0:T(8,128)S(1)} custom-call(bf16[128,8192]{1,0:T(8,128)(2,1)} %act_hbm.1, bf16[128,8192]{1,0:T(8,128)(2,1)} %q_hbm.1, bf16[128,1024]{1,0:T(8,128)(2,1)} %k_hbm.1, bf16[128,8192]{1,0:T(8,128)(2,1)} %grad_hbm.1, s32[8192]{0:T(1024)} %layout_hbm.1), custom_call_target="tpu_custom_call" | custom-call | tf_op jit(solution)/shard_map/pallas_call | solution.py:384
  53.8 1.0 %copy.7 = f32[256,1024]{1,0:T(8,128)} copy(f32[256,1024]{1,0:T(8,128)S(1)} %shard_map.55) | data formatting | bytes 2097152

commit v2 on v1

--- a/solution.py
+++ b/solution.py
@@ -37,7 +37,7 @@
     act_hbm, q_hbm, k_hbm, grad_hbm, layout_hbm, out_ref,
     act, flipped, picked, lay, qb, kb, gb, send, held, vg, down_in, up_in, part, acc,
     act_sem, lay_sem, load_sem, swap_send, swap_recv, a2a_send, a2a_recv, ag_send, ag_recv,
-    fwd_send, fwd_recv, rs_send, line_sem, *, planes, inner,
+    fwd_send, fwd_recv, rs_send, line_sem, end_sem, *, planes, inner,
 ):
     tokens, width = act_hbm.shape
     rows = out_ref.shape[0]
@@ -79,7 +79,7 @@
     ]
     lay_load = pltpu.make_async_copy(layout_hbm, lay, lay_sem)
     loads = [pltpu.make_async_copy(*cut(i, core), load_sem.at[i]) for i in range(len(cuts))]
-    for load in [*flips, lay_load, *loads]:
+    for load in [*flips, lay_load]:
         load.start()
 
     barrier = pltpu.get_barrier_semaphore()
@@ -96,8 +96,6 @@
         pl.semaphore_signal(barrier, inc=1, device_id=(me + inner, core), device_id_type=MESH)
 
     near = inner * SEQ - 1 + jnp.where(z > 0, 1, 0) + jnp.where(z < planes - 1, 1, 0)
-    with jax.named_scope('barrier'):
-        pl.semaphore_wait(barrier, near)
 
     swaps = []
     for i in range(len(cuts)):
@@ -108,10 +106,7 @@
                 device_id=(me, other), device_id_type=MESH,
             )
         )
-    for swap in swaps:
-        swap.start()
-
-    step = 512
+    step = 1024
 
     def flip(i, carry):
         at = pl.multiple_of(i * step, step)
@@ -121,8 +116,16 @@
     for i, load in enumerate(flips):
         with jax.named_scope("act_wait"):
             load.wait()
+        if i == 0:
+            for other_load in loads:
+                other_load.start()
         with jax.named_scope("flip"):
             lax.fori_loop(i * stretch // step, (i + 1) * stretch // step, flip, 0)
+        if i == 1:
+            with jax.named_scope("barrier"):
+                pl.semaphore_wait(barrier, near)
+            for swap in swaps:
+                swap.start()
     lay_load.wait()
 
     def wait_for(like, sem):
@@ -196,10 +199,10 @@
             axis=0,
         )
 
-    def grads(from_p, from_core, g):
+    def grads(from_p, at):
         return vg.at[
             pl.ds(pl.multiple_of(from_p * length, 128), length),
-            pl.ds(pl.multiple_of((g * SEQ + from_core) * HD, 128), HD),
+            pl.ds(pl.multiple_of(at * HD, 128), HD),
         ]
 
     def attend(g):
@@ -226,19 +229,19 @@
                 weights_of(second), stacked(gb, tokens, col), preferred_element_type=jnp.float32
             )
         done = jnp.concatenate([both[:tokens] + early, both[tokens:]], axis=0)
-        grads(p, core, g)[...] = done.astype(jnp.bfloat16)
+        grads(p, 2 * g)[...] = done.astype(jnp.bfloat16)
 
     def gather_copy(g, jp):
         return pltpu.make_async_remote_copy(
-            src_ref=grads(p, core, g), dst_ref=grads(p, core, g),
+            src_ref=grads(p, 2 * g), dst_ref=grads(p, 2 * g),
             send_sem=ag_send, recv_sem=ag_recv.at[g],
             device_id=(z * inner + relative(p, jp, bits), core), device_id_type=MESH,
         )
 
     def forward_copy(g, jp):
-        piece = grads(relative(p, jp, bits), core, g)
+        from_p = relative(p, jp, bits)
         return pltpu.make_async_remote_copy(
-            src_ref=piece, dst_ref=piece,
+            src_ref=grads(from_p, 2 * g), dst_ref=grads(from_p, 2 * g + 1),
             send_sem=fwd_send, recv_sem=fwd_recv.at[g],
             device_id=(me, other), device_id_type=MESH,
         )
@@ -257,61 +260,80 @@
     def arrived(g):
         wait_for(vg.at[:, :HD], fwd_recv.at[g])
 
-    def slot(ref, owner, h, g):
+    def slot(ref, owner, h, at, wide):
         return ref.at[
             owner,
             pl.ds(pl.multiple_of(h * half, 16), half),
-            pl.ds(pl.multiple_of(g * SEQ * HD, 128), SEQ * HD),
+            pl.ds(pl.multiple_of(at * HD, 128), wide * HD),
         ]
 
-    def up_copy(owner, h, g):
+    def up_copy(owner, h, at, wide):
+        sem = end_sem.at[1, h, at] if wide == 1 else line_sem.at[owner - 1, h, at // 2]
         return pltpu.make_async_remote_copy(
-            src_ref=slot(part, owner, h, g), dst_ref=slot(up_in, owner, h, g),
-            send_sem=rs_send, recv_sem=line_sem.at[owner, h, g],
+            src_ref=slot(part, owner, h, at, wide), dst_ref=slot(up_in, owner, h, at, wide),
+            send_sem=rs_send, recv_sem=sem,
             device_id=(me + inner, core), device_id_type=MESH,
         )
 
-    def down_copy(owner, h, g, at):
+    def down_copy(owner, h, at, wide, to):
+        if wide == 1:
+            sem = end_sem.at[0, h, at]
+        else:
+            sem = line_sem.at[jnp.where(owner == to, planes, owner) - 1 - jnp.where(owner == to, 1, 0), h, at // 2]
         return pltpu.make_async_remote_copy(
-            src_ref=slot(part, owner, h, g), dst_ref=slot(down_in, owner, h, g),
-            send_sem=rs_send, recv_sem=line_sem.at[jnp.where(owner == at, planes, owner), h, g],
+            src_ref=slot(part, owner, h, at, wide), dst_ref=slot(down_in, owner, h, at, wide),
+            send_sem=rs_send, recv_sem=sem,
             device_id=(me - inner, core), device_id_type=MESH,
         )
 
-    def reduce(k, h, g):
+    def reduce(k, h, at, wide):
         owner = turn(z, k, planes)
         at_rows = pl.ds(pl.multiple_of(h * half, 16), half)
-        cols = pl.ds(pl.multiple_of(g * SEQ * HD, 128), SEQ * HD)
-        acc[...] = jnp.dot(held[owner, at_rows, :], vg[:, cols], preferred_element_type=jnp.float32)
+        cols = pl.ds(pl.multiple_of(at * HD, 128), wide * HD)
+        here = acc.at[:, : wide * HD]
+        here[...] = jnp.dot(held[owner, at_rows, :], vg[:, cols], preferred_element_type=jnp.float32)
 
         @pl.when((owner >= z) & (z > 0))
         def _():
-            up_copy(owner, h, g).wait_recv()
-            acc[...] += slot(up_in, owner, h, g)[...].astype(jnp.float32)
+            up_copy(owner, h, at, wide).wait_recv()
+            here[...] += slot(up_in, owner, h, at, wide)[...].astype(jnp.float32)
 
         @pl.when((owner <= z) & (z < planes - 1))
         def _():
-            down_copy(owner, h, g, z).wait_recv()
-            acc[...] += slot(down_in, owner, h, g)[...].astype(jnp.float32)
+            down_copy(owner, h, at, wide, z).wait_recv()
+            here[...] += slot(down_in, owner, h, at, wide)[...].astype(jnp.float32)
 
         @pl.when(owner == z)
         def _():
-            for c in range(SEQ):
-                out_ref[at_rows, pl.ds(pl.multiple_of((c * groups + g) * HD, 128), HD)] = acc[
+            for c in range(wide):
+                of_core = (core + at + c) % SEQ
+                out_ref[at_rows, pl.ds(pl.multiple_of((of_core * groups + (at + c) // 2) * HD, 128), HD)] = acc[
                     :, c * HD : (c + 1) * HD
                 ]
 
         @pl.when(owner != z)
         def _():
-            slot(part, owner, h, g)[...] = acc[...].astype(jnp.bfloat16)
+            slot(part, owner, h, at, wide)[...] = here[...].astype(jnp.bfloat16)
 
         @pl.when(owner > z)
         def _():
-            up_copy(owner, h, g).start()
+            up_copy(owner, h, at, wide).start()
 
         @pl.when(owner < z)
         def _():
-            down_copy(owner, h, g, z - 1).start()
+            down_copy(owner, h, at, wide, z - 1).start()
+
+    def reduce_all(k, h):
+        owner = turn(z, k, planes)
+        at_end = (owner == 0) | (owner == planes - 1)
+
+        @pl.when(at_end)
+        def _():
+            each(0, 2 * groups, lambda at: reduce(k, h, at, 1))
+
+        @pl.when(jnp.logical_not(at_end))
+        def _():
+            each(0, groups, lambda g: reduce(k, h, 2 * g, 2))
 
     def each(first, last, step):
         lax.fori_loop(first, last, lambda i, carry: (step(i), carry)[1], 0)
@@ -332,33 +354,50 @@
         wait_for(qb.at[:, group_cols:], swap_recv.at[1])
     with jax.named_scope("a123"):
         each(1, groups, publish)
+    later = [lambda i=i: gather(i // 2, i % 2) for i in range(2, 2 * planes)]
+
+    def next_gather():
+        if later:
+            with jax.named_scope("gnext"):
+                later.pop(0)()
+
+    next_gather()
     for g in range(groups):
         with jax.named_scope(f"pass{g}"):
             pass_on(g)
-        if g < 2 * (planes - 1):
-            with jax.named_scope(f"ga{g}"):
-                gather(1 + g // 2, g % 2)
         if g == 0:
             with jax.named_scope("took00"):
                 took(0, 0)
+        with jax.named_scope(f"red0_{g}own"):
+            reduce(0, 0, 2 * g, 1)
+            if g:
+                reduce(0, 1, 2 * g, 1)
+        if g == 0:
+            next_gather()
         with jax.named_scope(f"arr{g}"):
             arrived(g)
-        with jax.named_scope(f"red0_{g}"):
-            reduce(0, 0, g)
+        with jax.named_scope(f"red0_{g}other"):
+            reduce(0, 0, 2 * g + 1, 1)
             if g == 0:
                 with jax.named_scope("took01"):
                     took(0, 1)
-            reduce(0, 1, g)
-    with jax.named_scope("glast"):
-        each(groups, 2 * (planes - 1), lambda i: gather(1 + i // 2, i % 2))
+                reduce(0, 1, 0, 1)
+            reduce(0, 1, 2 * g + 1, 1)
+        if g == 0:
+            next_gather()
+        if g < groups - 1:
+            next_gather()
 
     def rest(i):
         with jax.named_scope("took"):
             took(i // 2, i % 2)
         with jax.named_scope("red"):
-            each(0, groups, lambda g: reduce(i // 2, i % 2, g))
-
-    each(2, 2 * planes, rest)
+            reduce_all(i // 2, i % 2)
+
+    rest(2)
+    with jax.named_scope("glast"):
+        each(2 * planes - len(later), 2 * planes, lambda i: gather(i // 2, i % 2))
+    each(3, 2 * planes, rest)
 
     with jax.named_scope("t0"):
         for ref in (qb, gb, kb):
@@ -413,7 +452,8 @@
             dma(()),
             dma((groups,)),
             dma(()),
-            dma((planes + 1, 2, groups)),
+            dma((planes - 1, 2, groups)),
+            dma((2, 2, 2 * groups)),
         ],
         compiler_params=pltpu.CompilerParams(
             collective_id=0, has_side_effects=True, vmem_limit_bytes=32 * 2**20

time: 55.2 us -> 53.2 us (0.964)
  Pallas kernels: 53.8 us -> 52 us
    pallas_call x1, Pallas kernels: 53.8 us -> 52 us  [body(): pl.pallas_call(functools.partial(fused_kernel, planes=planes, inner=inner...]
where the time goes in v2:
time: 53.2 us; the launch traced here: 53 us
  Pallas kernels  52 us (98%)
  local copies, waits for them, and re-layouts  0.97 us (2%)
    pallas_call x1, Pallas kernels, body(): pl.pallas_call(functools.partial(fused_kernel, planes=planes, inner=inner...  52 us

profile of v2, /device:TPU:17, one launch (start us, length us, event | category | flops | bytes accessed | tf_op | source)
XLA Modules:
  0.0 53.0 jit_solution(16530144565291419629)
XLA Ops:
  0.0 52.0 %shard_map.55 = f32[256,1024]{1,0:T(8,128)S(1)} custom-call(bf16[128,8192]{1,0:T(8,128)(2,1)} %act_hbm.1, bf16[128,8192]{1,0:T(8,128)(2,1)} %q_hbm.1, bf16[128,1024]{1,0:T(8,128)(2,1)} %k_hbm.1, bf16[128,8192]{1,0:T(8,128)(2,1)} %grad_hbm.1, s32[8192]{0:T(1024)} %layout_hbm.1), custom_call_target="tpu_custom_call" | custom-call | tf_op jit(solution)/shard_map/pallas_call | solution.py:423
  52.0 1.0 %copy.7 = f32[256,1024]{1,0:T(8,128)} copy(f32[256,1024]{1,0:T(8,128)S(1)} %shard_map.55) | data formatting | bytes 2097152

commit v3 on v2

--- a/solution.py
+++ b/solution.py
@@ -78,7 +78,7 @@
         for i in range(width // stretch)
     ]
     lay_load = pltpu.make_async_copy(layout_hbm, lay, lay_sem)
-    loads = [pltpu.make_async_copy(*cut(i, core), load_sem.at[i]) for i in range(len(cuts))]
+    loads = [pltpu.make_async_copy(*cut(i, core), load_sem.at[int(i >= early_cuts)]) for i in range(len(cuts))]
     for load in [*flips, lay_load]:
         load.start()
 
@@ -168,7 +168,8 @@
         def first_row(to_p, to_core):
             return ((owner * inner + to_p) * SEQ + to_core) * rows + h * half
 
-        def to(j, carry):
+        def to(i, carry):
+            j = inner * SEQ - i
             pick(first_row(relative(p, j // SEQ, bits), (core + j) % SEQ))
             send[k, j, pl.ds(pl.multiple_of(h * half, 16), half)] = picked[...].astype(jnp.bfloat16)
             block(k, h, j).start()
@@ -248,7 +249,7 @@
 
     def publish(g):
         attend(g)
-        for jp in range(1, inner):
+        for jp in reversed(range(1, inner)):
             gather_copy(g, jp).start()
         forward_copy(g, 0).start()
 
@@ -261,14 +262,15 @@
         wait_for(vg.at[:, :HD], fwd_recv.at[g])
 
     def slot(ref, owner, h, at, wide):
-        return ref.at[
-            owner,
-            pl.ds(pl.multiple_of(h * half, 16), half),
-            pl.ds(pl.multiple_of(at * HD, 128), wide * HD),
-        ]
+        count = rows if h is None else half
+        first = 0 if h is None else pl.multiple_of(h * half, 16)
+        return ref.at[owner, pl.ds(first, count), pl.ds(pl.multiple_of(at * HD, 128), wide * HD)]
+
+    def end_sem_of(end, h, at):
+        return end_sem.at[end, at if h is None or h == 0 else 2 * groups + at]
 
     def up_copy(owner, h, at, wide):
-        sem = end_sem.at[1, h, at] if wide == 1 else line_sem.at[owner - 1, h, at // 2]
+        sem = end_sem_of(1, h, at) if wide == 1 else line_sem.at[owner - 1, h, at // 2]
         return pltpu.make_async_remote_copy(
             src_ref=slot(part, owner, h, at, wide), dst_ref=slot(up_in, owner, h, at, wide),
             send_sem=rs_send, recv_sem=sem,
@@ -277,7 +279,7 @@
 
     def down_copy(owner, h, at, wide, to):
         if wide == 1:
-            sem = end_sem.at[0, h, at]
+            sem = end_sem_of(0, h, at)
         else:
             sem = line_sem.at[jnp.where(owner == to, planes, owner) - 1 - jnp.where(owner == to, 1, 0), h, at // 2]
         return pltpu.make_async_remote_copy(
@@ -288,9 +290,10 @@
 
     def reduce(k, h, at, wide):
         owner = turn(z, k, planes)
-        at_rows = pl.ds(pl.multiple_of(h * half, 16), half)
+        count = rows if h is None else half
+        at_rows = pl.ds(0 if h is None else pl.multiple_of(h * half, 16), count)
         cols = pl.ds(pl.multiple_of(at * HD, 128), wide * HD)
-        here = acc.at[:, : wide * HD]
+        here = acc.at[:count, : wide * HD]
         here[...] = jnp.dot(held[owner, at_rows, :], vg[:, cols], preferred_element_type=jnp.float32)
 
         @pl.when((owner >= z) & (z > 0))
@@ -308,7 +311,7 @@
             for c in range(wide):
                 of_core = (core + at + c) % SEQ
                 out_ref[at_rows, pl.ds(pl.multiple_of((of_core * groups + (at + c) // 2) * HD, 128), HD)] = acc[
-                    :, c * HD : (c + 1) * HD
+                    :count, c * HD : (c + 1) * HD
                 ]
 
         @pl.when(owner != z)
@@ -323,17 +326,13 @@
         def _():
             down_copy(owner, h, at, wide, z - 1).start()
 
-    def reduce_all(k, h):
+    def reduce_both(k):
+        each(0, 2, lambda at: [reduce(k, h, at, 1) for h in range(2)])
+        each(2, 2 * groups, lambda at: reduce(k, None, at, 1))
+
+    def at_end(k):
         owner = turn(z, k, planes)
-        at_end = (owner == 0) | (owner == planes - 1)
-
-        @pl.when(at_end)
-        def _():
-            each(0, 2 * groups, lambda at: reduce(k, h, at, 1))
-
-        @pl.when(jnp.logical_not(at_end))
-        def _():
-            each(0, groups, lambda g: reduce(k, h, 2 * g, 2))
+        return (owner == 0) | (owner == planes - 1)
 
     def each(first, last, step):
         lax.fori_loop(first, last, lambda i, carry: (step(i), carry)[1], 0)
@@ -341,17 +340,15 @@
     with jax.named_scope("g00"):
         gather(0, 0)
     with jax.named_scope("qwait"):
-        for load in loads[:early_cuts]:
-            load.wait()
-        wait_for(qb.at[:tokens, : 2 * group_cols + key_cols], swap_recv.at[0])
+        for sem in (load_sem, swap_recv):
+            wait_for(qb.at[:tokens, : 2 * group_cols + key_cols], sem.at[0])
     with jax.named_scope("a0"):
         publish(0)
     with jax.named_scope("g01"):
         gather(0, 1)
     with jax.named_scope("qwait2"):
-        for load in loads[early_cuts:]:
-            load.wait()
-        wait_for(qb.at[:, group_cols:], swap_recv.at[1])
+        for sem in (load_sem, swap_recv):
+            wait_for(qb.at[:, group_cols:], sem.at[1])
     with jax.named_scope("a123"):
         each(1, groups, publish)
     later = [lambda i=i: gather(i // 2, i % 2) for i in range(2, 2 * planes)]
@@ -361,7 +358,6 @@
             with jax.named_scope("gnext"):
                 later.pop(0)()
 
-    next_gather()
     for g in range(groups):
         with jax.named_scope(f"pass{g}"):
             pass_on(g)
@@ -369,35 +365,45 @@
             with jax.named_scope("took00"):
                 took(0, 0)
         with jax.named_scope(f"red0_{g}own"):
-            reduce(0, 0, 2 * g, 1)
-            if g:
-                reduce(0, 1, 2 * g, 1)
+            reduce(0, None if g else 0, 2 * g, 1)
         if g == 0:
             next_gather()
         with jax.named_scope(f"arr{g}"):
             arrived(g)
         with jax.named_scope(f"red0_{g}other"):
-            reduce(0, 0, 2 * g + 1, 1)
+            reduce(0, None if g else 0, 2 * g + 1, 1)
             if g == 0:
                 with jax.named_scope("took01"):
                     took(0, 1)
                 reduce(0, 1, 0, 1)
-            reduce(0, 1, 2 * g + 1, 1)
+                reduce(0, 1, 1, 1)
         if g == 0:
             next_gather()
         if g < groups - 1:
             next_gather()
 
-    def rest(i):
-        with jax.named_scope("took"):
-            took(i // 2, i % 2)
-        with jax.named_scope("red"):
-            reduce_all(i // 2, i % 2)
-
-    rest(2)
-    with jax.named_scope("glast"):
-        each(2 * planes - len(later), 2 * planes, lambda i: gather(i // 2, i % 2))
-    each(3, 2 * planes, rest)
+    def rest(k, between=None):
+        def half_of(h):
+            with jax.named_scope("took"):
+                took(k, h)
+
+            @pl.when(jnp.logical_not(at_end(k)))
+            def _():
+                with jax.named_scope("red"):
+                    each(0, groups, lambda g: reduce(k, h, 2 * g, 2))
+
+        half_of(0)
+        if between is not None:
+            between()
+        half_of(1)
+
+        @pl.when(at_end(k))
+        def _():
+            with jax.named_scope("redend"):
+                reduce_both(k)
+
+    rest(1, lambda: each(2 * planes - len(later), 2 * planes, lambda i: gather(i // 2, i % 2)))
+    each(2, planes, rest)
 
     with jax.named_scope("t0"):
         for ref in (qb, gb, kb):
@@ -439,13 +445,13 @@
             pltpu.VMEM((planes, rows, kv_width), jnp.bfloat16),
             pltpu.VMEM((planes, rows, kv_width), jnp.bfloat16),
             pltpu.VMEM((planes, rows, kv_width), jnp.bfloat16),
-            pltpu.VMEM((rows // 2, SEQ * HD), jnp.float32),
+            pltpu.VMEM((rows, SEQ * HD), jnp.float32),
             dma((4,)),
             dma(()),
-            dma((5,)),
-            dma(()),
             dma((2,)),
             dma(()),
+            dma((2,)),
+            dma(()),
             dma((planes, 2)),
             dma(()),
             dma((groups,)),
@@ -453,7 +459,7 @@
             dma((groups,)),
             dma(()),
             dma((planes - 1, 2, groups)),
-            dma((2, 2, 2 * groups)),
+            dma((2, 2 * groups + 2)),
         ],
         compiler_params=pltpu.CompilerParams(
             collective_id=0, has_side_effects=True, vmem_limit_bytes=32 * 2**20

time: 53.2 us -> 52.6 us (0.989)
    pallas_call x1, Pallas kernels: 52 us -> 51.5 us  [body(): pl.pallas_call(functools.partial(fused_kernel, planes=planes, inner=inner...]
where the time goes in v3:
time: 52.6 us; the launch traced here: 52.5 us
  Pallas kernels  51.5 us (98%)
  local copies, waits for them, and re-layouts  0.97 us (2%)
    pallas_call x1, Pallas kernels, body(): pl.pallas_call(functools.partial(fused_kernel, planes=planes, inner=inner...  51.5 us

profile of v3, /device:TPU:17, one launch (start us, length us, event | category | flops | bytes accessed | tf_op | source)
XLA Modules:
  0.0 52.5 jit_solution(9632447199533662119)
XLA Ops:
  0.0 51.5 %shard_map.55 = f32[256,1024]{1,0:T(8,128)S(1)} custom-call(bf16[128,8192]{1,0:T(8,128)(2,1)} %act_hbm.1, bf16[128,8192]{1,0:T(8,128)(2,1)} %q_hbm.1, bf16[128,1024]{1,0:T(8,128)(2,1)} %k_hbm.1, bf16[128,8192]{1,0:T(8,128)(2,1)} %grad_hbm.1, s32[8192]{0:T(1024)} %layout_hbm.1), custom_call_target="tpu_custom_call" | custom-call | tf_op jit(solution)/shard_map/pallas_call | solution.py:429
  51.5 1.0 %copy.7 = f32[256,1024]{1,0:T(8,128)} copy(f32[256,1024]{1,0:T(8,128)S(1)} %shard_map.55) | data formatting | bytes 2097152

commit v4 on v1

v4 whole, which is shorter than its diff:
```python
import functools
import math

import jax
import jax.numpy as jnp
from jax import lax
from jax.experimental import pallas as pl
from jax.experimental.pallas import tpu as pltpu
from jax.sharding import PartitionSpec as P

H = 64
KVH = 8
HD = 128
SEQ = 2
MESH = pl.DeviceIdType.MESH


def relative(place, step, bits):
    total = 0
    for b in range(bits):
        total = total + (place // (1 << b) + step // (1 << b)) % 2 * (1 << b)
    return total


def fused_kernel(
    act_hbm, q_hbm, k_hbm, grad_hbm, layout_hbm, out_ref,
    act, flipped, picked, lay, qb, kb, gb, send, held, vg, line_in, part, acc,
    act_sem, lay_sem, load_sem, swap_send, swap_recv, a2a_send, a2a_recv, ag_send, ag_recv,
    fwd_send, fwd_recv, rs_send, line_sem, *, group_masks, line_masks,
):
    tokens, width = act_hbm.shape
    rows = out_ref.shape[0]
    bits = len(group_masks) + len(line_masks)
    inner, sets = 1 << len(group_masks), 1 << len(line_masks)
    me, core = lax.axis_index("dp"), lax.axis_index("seq")
    other = 1 - core
    heads_cols, key_cols = q_hbm.shape[1] // SEQ, k_hbm.shape[1] // SEQ
    length = SEQ * tokens
    per_group = H // KVH
    groups = key_cols // HD
    half = rows // 2
    group_cols = per_group * HD
    stretch = width // 4

    moves = [mask * (1 - me // mask % 2 * 2) for mask in group_masks]

    def member(step):
        return me + sum(step // (1 << i) % 2 * move for i, move in enumerate(moves))

    def across(place, step):
        for i, mask in enumerate(line_masks):
            if step >> i & 1:
                for b in range(bits):
                    if mask >> b & 1:
                        place = place + (1 << b) * (1 - place // (1 << b) % 2 * 2)
        return place

    here_at = sum(me // mask % 2 * (1 << i) for i, mask in enumerate(group_masks))
    place = here_at * SEQ + core

    cuts = ((k_hbm, kb, key_cols, 0, key_cols),) + tuple(
        (source, target, heads_cols, first, last - first)
        for first, last in ((0, group_cols), (group_cols, heads_cols))
        for source, target in ((q_hbm, qb), (grad_hbm, gb))
    )

    early_cuts = 3

    def cut(i, of_core):
        source, target, cols, first, count = cuts[i]
        return (
            source.at[:, pl.ds(pl.multiple_of(of_core * cols + first, 128), count)],
            target.at[pl.ds(pl.multiple_of(core * tokens, 128), tokens), pl.ds(first, count)],
        )

    flips = [
        pltpu.make_async_copy(
            act_hbm.at[:, pl.ds(i * stretch, stretch)],
            act.at[:, pl.ds(i * stretch, stretch)],
            act_sem.at[i],
        )
        for i in range(width // stretch)
    ]
    lay_load = pltpu.make_async_copy(layout_hbm, lay, lay_sem)
    loads = [pltpu.make_async_copy(*cut(i, core), load_sem.at[int(i >= early_cuts)]) for i in range(len(cuts))]
    for load in [*flips, lay_load]:
        load.start()

    barrier = pltpu.get_barrier_semaphore()
    peers = [(member(j // SEQ), (core + j) % SEQ) for j in range(1, inner * SEQ)]
    peers += [(across(me, 1 << i), core) for i in range(len(line_masks))]
    for to in peers:
        pl.semaphore_signal(barrier, inc=1, device_id=to, device_id_type=MESH)

    swaps = []
    for i in range(len(cuts)):
        source, target = cut(i, other)
        swaps.append(
            pltpu.make_async_remote_copy(
                src_ref=source, dst_ref=target, send_sem=swap_send, recv_sem=swap_recv.at[int(i >= early_cuts)],
                device_id=(me, other), device_id_type=MESH,
            )
        )
    step = 2048

    def flip(i, carry):
        at = pl.multiple_of(i * step, step)
        flipped[pl.ds(at, step), :] = act[:, pl.ds(at, step)].T.astype(jnp.float32)
        return carry

    for i, load in enumerate(flips):
        with jax.named_scope("act_wait"):
            load.wait()
        if i == 0:
            for other_load in loads:
                other_load.start()
        with jax.named_scope("flip"):
            lax.fori_loop(i * stretch // step, (i + 1) * stretch // step, flip, 0)
        if i == 1:
            with jax.named_scope("barrier"):
                pl.semaphore_wait(barrier, len(peers))
            for swap in swaps:
                swap.start()
    lay_load.wait()

    def wait_for(like, sem):
        pltpu.make_async_remote_copy(
            src_ref=like, dst_ref=like, send_sem=sem, recv_sem=sem,
            device_id=(me, other), device_id_type=MESH,
        ).wait_recv()

    def pick(first_row):
        def some(i, carry):
            first = pl.multiple_of(i * 32, 32)
            for r in range(32):
                row = lay[first_row + first + r]
                picked[pl.ds(first + r, 1), :] = flipped[pl.ds(row, 1), :]
            return carry

        lax.fori_loop(0, half // 32, some, 0)

    def held_piece(s, h):
        return held.at[
            s,
            pl.ds(pl.multiple_of(h * half, 16), half),
            pl.ds(pl.multiple_of(place * tokens, 128), tokens),
        ]

    def block(s, h, j):
        return pltpu.make_async_remote_copy(
            src_ref=send.at[s, j, pl.ds(pl.multiple_of(h * half, 16), half)],
            dst_ref=held_piece(s, h),
            send_sem=a2a_send,
            recv_sem=a2a_recv.at[s, h],
            device_id=(member(j // SEQ), (core + j) % SEQ),
            device_id_type=MESH,
        )

    def gather(s, h, start=True):
        def first_row(j):
            owner = across(member(j // SEQ), s)
            return (owner * SEQ + (core + j) % SEQ) * rows + h * half

        def to(i, carry):
            j = inner * SEQ - i
            pick(first_row(j))
            send[s, j, pl.ds(pl.multiple_of(h * half, 16), half)] = picked[...].astype(jnp.bfloat16)
            if start:
                block(s, h, j).start()
            return carry

        lax.fori_loop(1, inner * SEQ, to, 0)
        pick(first_row(0))
        held_piece(s, h)[...] = picked[...].astype(jnp.bfloat16)

    def release(s, h):
        lax.fori_loop(1, inner * SEQ, lambda i, carry: (block(s, h, inner * SEQ - i).start(), carry)[1], 0)

    def took(s, h):
        wait_for(send.at[0, 1:, :half], a2a_recv.at[s, h])

    scale = math.log2(math.e) / float(HD) ** 0.5
    key_at = lax.broadcasted_iota(jnp.int32, (tokens, 2 * tokens), 0)
    query_at = lax.broadcasted_iota(jnp.int32, (tokens, 2 * tokens), 1) % tokens
    allowed = key_at <= query_at

    def weights_of(scores):
        powers = jnp.exp2((scores - jnp.max(scores, axis=0, keepdims=True)) * scale)
        return (powers * (1.0 / jnp.sum(powers, axis=0, keepdims=True))).astype(jnp.bfloat16)

    def stacked(ref, row, col):
        return jnp.concatenate(
            [
                ref[row : row + tokens, pl.ds(pl.multiple_of(col, 128), HD)],
                ref[row : row + tokens, pl.ds(pl.multiple_of(col + HD, 128), HD)],
            ],
            axis=0,
        )

    def attend(g):
        keys = kb[:, pl.ds(pl.multiple_of(g * HD, 128), HD)]
        early = jnp.zeros((tokens, HD), jnp.float32)
        both = jnp.zeros((length, HD), jnp.float32)
        for pair in range(per_group // 2):
            col = (g * per_group + 2 * pair) * HD
            against = (((1,), (1,)), ((), ()))
            first = lax.dot_general(
                keys[:tokens], stacked(qb, 0, col), against, preferred_element_type=jnp.float32
            )
            second = lax.dot_general(
                keys, stacked(qb, tokens, col), against, preferred_element_type=jnp.float32
            )
            first = jnp.where(allowed, first, -jnp.inf)
            second = jnp.concatenate(
                [second[:tokens], jnp.where(allowed, second[tokens:], -jnp.inf)], axis=0
            )
            early += jnp.dot(
                weights_of(first), stacked(gb, 0, col), preferred_element_type=jnp.float32
            )
            both += jnp.dot(
                weights_of(second), stacked(gb, tokens, col), preferred_element_type=jnp.float32
            )
        done = jnp.concatenate([both[:tokens] + early, both[tokens:]], axis=0)
        grads(0, 2 * g)[...] = done.astype(jnp.bfloat16)

    def grads(step, at):
        from_at = relative(here_at, step, len(group_masks))
        return vg.at[
            pl.ds(pl.multiple_of(from_at * length, 128), length),
            pl.ds(pl.multiple_of(at * HD, 128), HD),
        ]

    def gather_copy(g, step, i):
        return pltpu.make_async_remote_copy(
            src_ref=grads(step, 2 * g), dst_ref=grads(step, 2 * g),
            send_sem=ag_send, recv_sem=ag_recv.at[g, step + (1 << i)],
            device_id=(member(1 << i), core), device_id_type=MESH,
        )

    def forward_copy(g, step):
        return pltpu.make_async_remote_copy(
            src_ref=grads(step, 2 * g), dst_ref=grads(step, 2 * g + 1),
            send_sem=fwd_send, recv_sem=fwd_recv.at[g],
            device_id=(me, other), device_id_type=MESH,
        )

    def direct_copy(g, step):
        return pltpu.make_async_remote_copy(
            src_ref=grads(0, 2 * g), dst_ref=grads(0, 2 * g),
            send_sem=ag_send, recv_sem=ag_recv.at[g, step],
            device_id=(member(step), core), device_id_type=MESH,
        )

    def publish(g, direct=False):
        attend(g)
        if direct:
            for step in reversed(range(1, inner)):
                direct_copy(g, step).start()
        else:
            for i in reversed(range(len(group_masks))):
                gather_copy(g, 0, i).start()
        forward_copy(g, 0).start()

    def pass_on(g, step, relay=True):
        wait_for(vg.at[:length, :HD], ag_recv.at[g, step])
        lowest = (step & -step).bit_length() - 1
        if relay:
            for i in reversed(range(lowest)):
                gather_copy(g, step, i).start()
        forward_copy(g, step).start()

    near_steps = [1 << i for i in reversed(range(len(group_masks)))]
    far_steps = sorted(
        (step for step in range(1, inner) if step not in near_steps), key=lambda step: (bin(step).count("1"), -step)
    )

    def arrived(g):
        wait_for(vg.at[:, :HD], fwd_recv.at[g])

    def slot(ref, s, h, g):
        return ref.at[
            s,
            pl.ds(pl.multiple_of(h * half, 16), half),
            pl.ds(pl.multiple_of(g * SEQ * HD, 128), SEQ * HD),
        ]

    def line_copy(s, h, g):
        lowest = (s & -s).bit_length() - 1
        return pltpu.make_async_remote_copy(
            src_ref=slot(part, s - 1, h, g), dst_ref=slot(line_in, s - 1, h, g),
            send_sem=rs_send, recv_sem=line_sem.at[s - 1, h, g],
            device_id=(across(me, 1 << lowest), core), device_id_type=MESH,
        )

    def reduce(s, h, g):
        at_rows = pl.ds(pl.multiple_of(h * half, 16), half)
        cols = pl.ds(pl.multiple_of(g * SEQ * HD, 128), SEQ * HD)
        acc[...] = jnp.dot(held[s, at_rows, :], vg[:, cols], preferred_element_type=jnp.float32)
        lowest = (s & -s).bit_length() - 1 if s else len(line_masks)
        for i in range(lowest):
            line_copy(s + (1 << i), h, g).wait_recv()
            acc[...] += slot(line_in, s + (1 << i) - 1, h, g)[...].astype(jnp.float32)
        if s:
            slot(part, s - 1, h, g)[...] = acc[...].astype(jnp.bfloat16)
            line_copy(s, h, g).start()
        else:
            for c in range(SEQ):
                of_core = (core + c) % SEQ
                out_ref[at_rows, pl.ds(pl.multiple_of((of_core * groups + g) * HD, 128), HD)] = acc[
                    :, c * HD : (c + 1) * HD
                ]

    def each(first, last, step):
        lax.fori_loop(first, last, lambda i, carry: (step(i), carry)[1], 0)

    order = [(sets - 1, 0), (sets - 2, 0), (sets - 1, 1), (sets - 2, 1)]
    order += [(s, h) for s in reversed(range(sets - 2)) for h in range(2)]
    later = order[3:]

    def next_gather():
        if later:
            with jax.named_scope("gnext"):
                gather(*later.pop(0))

    def pass_near(g):
        with jax.named_scope(f"pass{g}"):
            for step in near_steps:
                pass_on(g, step)

    def pass_far(g):
        with jax.named_scope(f"far{g}"):
            for step in far_steps:
                pass_on(g, step)

    def first(g):
        with jax.named_scope(f"arr{g}"):
            arrived(g)
        with jax.named_scope(f"redfirst{g}"):
            reduce(sets - 1, 0, g)

    def second(g):
        with jax.named_scope(f"redsecond{g}"):
            reduce(sets - 2, 0, g)

    with jax.named_scope("g00"):
        gather(*order[0])
    with jax.named_scope("qwait"):
        for sem in (load_sem, swap_recv):
            wait_for(qb.at[:tokens, : 2 * group_cols + key_cols], sem.at[0])
    with jax.named_scope("a0"):
        publish(0, True)
    with jax.named_scope("g01"):
        gather(*order[1])
    for sem in (load_sem, swap_recv):
        wait_for(qb.at[:, group_cols:], sem.at[1])
    with jax.named_scope("a123"):
        each(1, groups, publish)
    with jax.named_scope("pass0"):
        for step in range(1, inner):
            pass_on(0, step, False)
    with jax.named_scope("held"):
        gather(*order[2], False)
    took(*order[0])
    first(0)
    for g in range(1, groups):
        pass_near(g)
        if g == 2:
            took(*order[1])
            second(0)
    release(*order[2])
    next_gather()
    pass_far(1)
    first(1)
    for g in range(2, groups):
        pass_far(g)
        next_gather()
        first(g)
        second(g - 1)

    def rest(s, h):
        with jax.named_scope("took"):
            took(s, h)
        with jax.named_scope(f"red{s}{h}"):
            each(0, groups, lambda g: reduce(s, h, g))

    rest(*order[2])
    second(groups - 1)
    while later:
        next_gather()
    rest(*order[3])
    for s, h in order[4:]:
        rest(s, h)

    with jax.named_scope("t0"):
        for ref in (qb, gb, kb):
            wait_for(ref.at[:tokens], swap_send)
        wait_for(send.at[:, 1:], a2a_send)
        wait_for(vg.at[: (inner - 1) * length, : groups * HD], ag_send)
        wait_for(vg.at[:, : groups * HD], fwd_send)
    with jax.named_scope("t3"):
        wait_for(part, rs_send)


def body(activations, queries, keys, out_grad, layout):
    members = lax.axis_size("dp")
    tokens, width = activations.shape
    bits = members.bit_length() - 1
    group_masks = [1 << b for b in range(0, bits, 2)]
    line_masks = [1 << b for b in range(1, bits, 2)]
    line_masks[-1] += line_masks[-1] // 2
    inner, sets = 1 << len(group_masks), 1 << len(line_masks)
    rows = layout.shape[0] // (members * SEQ)
    kv_width = keys.shape[1]
    groups = kv_width // SEQ // HD
    length = SEQ * tokens
    dma = pltpu.SemaphoreType.DMA
    operands = (activations, queries, keys, out_grad, layout)
    return pl.pallas_call(
        functools.partial(fused_kernel, group_masks=group_masks, line_masks=line_masks),
        out_shape=jax.ShapeDtypeStruct((rows, kv_width), jnp.float32),
        in_specs=[pl.BlockSpec(memory_space=pltpu.HBM)] * len(operands),
        out_specs=pl.BlockSpec(memory_space=pltpu.VMEM),
        scratch_shapes=[
            pltpu.VMEM((tokens, width), jnp.bfloat16),
            pltpu.VMEM((width, tokens), jnp.float32),
            pltpu.VMEM((rows // 2, tokens), jnp.float32),
            pltpu.SMEM(layout.shape, jnp.int32),
            pltpu.VMEM((length, queries.shape[1] // SEQ), jnp.bfloat16),
            pltpu.VMEM((length, kv_width // SEQ), jnp.bfloat16),
            pltpu.VMEM((length, queries.shape[1] // SEQ), jnp.bfloat16),
            pltpu.VMEM((sets, inner * SEQ, rows, tokens), jnp.bfloat16),
            pltpu.VMEM((sets, rows, inner * length), jnp.bfloat16),
            pltpu.VMEM((inner * length, kv_width), jnp.bfloat16),
            pltpu.VMEM((sets - 1, rows, kv_width), jnp.bfloat16),
            pltpu.VMEM((sets - 1, rows, kv_width), jnp.bfloat16),
            pltpu.VMEM((rows // 2, SEQ * HD), jnp.float32),
            dma((4,)),
            dma(()),
            dma((2,)),
            dma(()),
            dma((2,)),
            dma(()),
            dma((sets, 2)),
            dma(()),
            dma((groups, inner)),
            dma(()),
            dma((groups,)),
            dma(()),
            dma((sets - 1, 2, groups)),
        ],
        compiler_params=pltpu.CompilerParams(
            collective_id=0, has_side_effects=True, vmem_limit_bytes=32 * 2**20
        ),
    )(*(pltpu.with_memory_space_constraint(x, pltpu.HBM) for x in operands))


def solution(mesh):
    whole = ("dp", "seq")
    return jax.shard_map(
        body,
        mesh=mesh,
        in_specs=(P(whole, None),) * 4 + (P(),),
        out_specs=P(whole, None),
        check_vma=False,
    )
```

time: 55.2 us -> 52.5 us (0.951)
  the two profiles are of different devices: /device:TPU:17 before, /device:TPU:0 now
where the time goes in v4:
time: 52.5 us; the launch traced here: 52.3 us
  Pallas kernels  51.4 us (98%)
  local copies, waits for them, and re-layouts  0.97 us (2%)
    pallas_call x1, Pallas kernels, body(): pl.pallas_call(functools.partial(fused_kernel, group_masks=group_masks, l...  51.4 us

profile of v4, /device:TPU:0, one launch (start us, length us, event | category | flops | bytes accessed | tf_op | source)
XLA Modules:
  0.0 52.3 jit_solution(17506976645893489613)
XLA Ops:
  0.0 51.4 %shard_map.55 = f32[256,1024]{1,0:T(8,128)S(1)} custom-call(bf16[128,8192]{1,0:T(8,128)(2,1)} %act_hbm.1, bf16[128,8192]{1,0:T(8,128)(2,1)} %q_hbm.1, bf16[128,1024]{1,0:T(8,128)(2,1)} %k_hbm.1, bf16[128,8192]{1,0:T(8,128)(2,1)} %grad_hbm.1, s32[8192]{0:T(1024)} %layout_hbm.1), custom_call_target="tpu_custom_call" | custom-call | tf_op jit(solution)/shard_map/pallas_call | solution.py:418
  51.4 1.0 %copy.7 = f32[256,1024]{1,0:T(8,128)} copy(f32[256,1024]{1,0:T(8,128)S(1)} %shard_map.55) | data formatting | bytes 2097152

commit v5 on v3

--- a/solution.py
+++ b/solution.py
@@ -106,7 +106,7 @@
                 device_id=(me, other), device_id_type=MESH,
             )
         )
-    step = 1024
+    step = 2048
 
     def flip(i, carry):
         at = pl.multiple_of(i * step, step)
@@ -169,7 +169,7 @@
             return ((owner * inner + to_p) * SEQ + to_core) * rows + h * half
 
         def to(i, carry):
-            j = inner * SEQ - i
+            j = jnp.where(i <= 4, inner * SEQ - 1 - (i - 1) % 2 * 2 - (i - 1) // 2, inner * SEQ - i)
             pick(first_row(relative(p, j // SEQ, bits), (core + j) % SEQ))
             send[k, j, pl.ds(pl.multiple_of(h * half, 16), half)] = picked[...].astype(jnp.bfloat16)
             block(k, h, j).start()

time: 52.6 us -> 52.5 us (level)
  no operation moved by 1% of the time
where the time goes in v5:
time: 52.5 us; the launch traced here: 52.4 us
  Pallas kernels  51.4 us (98%)
  local copies, waits for them, and re-layouts  0.97 us (2%)
    pallas_call x1, Pallas kernels, body(): pl.pallas_call(functools.partial(fused_kernel, planes=planes, inner=inner...  51.4 us

profile of v5, /device:TPU:17, one launch (start us, length us, event | category | flops | bytes accessed | tf_op | source)
XLA Modules:
  0.0 52.4 jit_solution(17591151312786090357)
XLA Ops:
  0.0 51.4 %shard_map.55 = f32[256,1024]{1,0:T(8,128)S(1)} custom-call(bf16[128,8192]{1,0:T(8,128)(2,1)} %act_hbm.1, bf16[128,8192]{1,0:T(8,128)(2,1)} %q_hbm.1, bf16[128,1024]{1,0:T(8,128)(2,1)} %k_hbm.1, bf16[128,8192]{1,0:T(8,128)(2,1)} %grad_hbm.1, s32[8192]{0:T(1024)} %layout_hbm.1), custom_call_target="tpu_custom_call" | custom-call | tf_op jit(solution)/shard_map/pallas_call | solution.py:429
  51.4 1.0 %copy.7 = f32[256,1024]{1,0:T(8,128)} copy(f32[256,1024]{1,0:T(8,128)S(1)} %shard_map.55) | data formatting | bytes 2097152

commit v6 on v5

--- a/solution.py
+++ b/solution.py
@@ -52,7 +52,8 @@
     half = rows // 2
     place = p * SEQ + core
     group_cols = per_group * HD
-    stretch = width // 4
+    stretches = [width // 8, width // 8] + [width // 4] * 3
+    starts = [sum(stretches[:i]) for i in range(len(stretches))]
 
     cuts = ((k_hbm, kb, key_cols, 0, key_cols),) + tuple(
         (source, target, heads_cols, first, last - first)
@@ -71,11 +72,11 @@
 
     flips = [
         pltpu.make_async_copy(
-            act_hbm.at[:, pl.ds(i * stretch, stretch)],
-            act.at[:, pl.ds(i * stretch, stretch)],
+            act_hbm.at[:, pl.ds(at, count)],
+            act.at[:, pl.ds(at, count)],
             act_sem.at[i],
         )
-        for i in range(width // stretch)
+        for i, (at, count) in enumerate(zip(starts, stretches))
     ]
     lay_load = pltpu.make_async_copy(layout_hbm, lay, lay_sem)
     loads = [pltpu.make_async_copy(*cut(i, core), load_sem.at[int(i >= early_cuts)]) for i in range(len(cuts))]
@@ -106,13 +107,6 @@
                 device_id=(me, other), device_id_type=MESH,
             )
         )
-    step = 2048
-
-    def flip(i, carry):
-        at = pl.multiple_of(i * step, step)
-        flipped[pl.ds(at, step), :] = act[:, pl.ds(at, step)].T.astype(jnp.float32)
-        return carry
-
     for i, load in enumerate(flips):
         with jax.named_scope("act_wait"):
             load.wait()
@@ -120,8 +114,9 @@
             for other_load in loads:
                 other_load.start()
         with jax.named_scope("flip"):
-            lax.fori_loop(i * stretch // step, (i + 1) * stretch // step, flip, 0)
-        if i == 1:
+            at, count = starts[i], stretches[i]
+            flipped[at : at + count, :] = act[:, at : at + count].T.astype(jnp.float32)
+        if i == 2:
             with jax.named_scope("barrier"):
                 pl.semaphore_wait(barrier, near)
             for swap in swaps:
@@ -446,7 +441,7 @@
             pltpu.VMEM((planes, rows, kv_width), jnp.bfloat16),
             pltpu.VMEM((planes, rows, kv_width), jnp.bfloat16),
             pltpu.VMEM((rows, SEQ * HD), jnp.float32),
-            dma((4,)),
+            dma((5,)),
             dma(()),
             dma((2,)),
             dma(()),

time: 52.5 us -> 52.5 us (level)
  no operation moved by 1% of the time
where the time goes in v6:
time: 52.5 us; the launch traced here: 52.4 us
  Pallas kernels  51.4 us (98%)
  local copies, waits for them, and re-layouts  0.97 us (2%)
    pallas_call x1, Pallas kernels, body(): pl.pallas_call(functools.partial(fused_kernel, planes=planes, inner=inner...  51.4 us

profile of v6, /device:TPU:17, one launch (start us, length us, event | category | flops | bytes accessed | tf_op | source)
XLA Modules:
  0.0 52.4 jit_solution(5315148012493346265)
XLA Ops:
  0.0 51.4 %shard_map.55 = f32[256,1024]{1,0:T(8,128)S(1)} custom-call(bf16[128,8192]{1,0:T(8,128)(2,1)} %act_hbm.1, bf16[128,8192]{1,0:T(8,128)(2,1)} %q_hbm.1, bf16[128,1024]{1,0:T(8,128)(2,1)} %k_hbm.1, bf16[128,8192]{1,0:T(8,128)(2,1)} %grad_hbm.1, s32[8192]{0:T(1024)} %layout_hbm.1), custom_call_target="tpu_custom_call" | custom-call | tf_op jit(solution)/shard_map/pallas_call | solution.py:424
  51.4 1.0 %copy.7 = f32[256,1024]{1,0:T(8,128)} copy(f32[256,1024]{1,0:T(8,128)S(1)} %shard_map.55) | data formatting | bytes 2097152
